TPU v7x, 32 devices: a whole 2x2x4 slice. The times are simulated.
32 devices in a mesh: dp: 8 (over y, x, core), mp: 4 (over z).
Axes of the slice: x: 2, y: 2, z: 4, core: 2. Of those that a mesh axis runs over, the one named last changes fastest.
Arguments:
- attn_out: bfloat16 [8192, 8192], P('dp', 'mp'), may hold values from -6 to 6
- out_weight: bfloat16 [8192, 8192], P('dp'), may hold values from -0.09375 to 0.09375
- residual: bfloat16 [8, 1024, 8192], P(None, 'mp', 'dp'), may hold values from -6 to 6
Outputs:
- layer_out: bfloat16 [8, 1024, 8192], P(None, 'mp', 'dp')
All inputs are finite; a program needn't handle non-finite values.
Results may differ from a plain program's by a relative error of at most 0.001.
Values may be sent and summed in bfloat16 or wider, within the bound.
A program may use at most 192 MiB of HBM per device.

v0:
```python
import jax
import jax.numpy as jnp
from jax import lax
from jax.sharding import PartitionSpec as P


def shards(attn_out, out_weight, residual):
    by_rows = lax.all_to_all(attn_out, "mp", split_axis=0, concat_axis=1, tiled=True)
    columns = lax.all_to_all(out_weight, "dp", split_axis=1, concat_axis=0, tiled=True)
    projected = jnp.dot(
        lax.all_gather(by_rows, "dp", axis=0, tiled=True),
        columns,
        preferred_element_type=jnp.float32,
    )
    layer_out = residual.astype(jnp.float32) + projected.reshape(residual.shape)
    return layer_out.astype(jnp.bfloat16)


def solution(mesh):
    return jax.shard_map(
        shards,
        mesh=mesh,
        in_specs=(P("dp", "mp"), P("dp", None), P(None, "mp", "dp")),
        out_specs=P(None, "mp", "dp"),
        check_vma=False,
    )
```

profile of v0, /device:TPU:0, one launch (start us, length us, event | category | flops | bytes accessed | tf_op | source)
XLA Modules:
  0.0 492.3 jit_solution(1192712560543331920)
XLA Ops:
  6.5 0.0 all-gather.2.cloned.1.call-start
  6.5 99.5 %all_to_all.38 = bf16[4,256,2048]{2,1,0:T(8,128)(2,1)S(1)} all-to-all(bf16[4,256,2048]{2,1,0:T(8,128)(2,1)} %bitcast.21), channel_id=1, replica_groups=mesh['dp'=8,'mp'=4] {'mp'}, dimensions={0} | all-to-all | bytes 8388608 | tf_op jit(solution)/shard_map/all_to_all | solution.py:8
  106.0 2.3 copy.7
  108.3 0.0 all-gather.2.cloned.1.call-update
  108.4 9.0 %copy.9 = bf16[128,8,8,1024]{3,2,0,1:T(8,128)(2,1)S(1)} copy(bf16[128,8,8,1024]{3,2,1,0:T(8,128)(2,1)} %bitcast.17) | data formatting | bytes 33554432 | tf_op jit(solution)/shard_map/all_to_all | solution.py:9
  117.4 312.1 %all_to_all.39 = bf16[1024,8,1024]{2,0,1:T(8,128)(2,1)} all-to-all(bf16[1024,8,1024]{2,0,1:T(8,128)(2,1)S(1)} %bitcast.16), channel_id=1, replica_groups=mesh['dp'=8,'mp'=4] {'dp'}, dimensions={1} | all-to-all | bytes 33554432 | tf_op jit(solution)/shard_map/all_to_all | solution.py:9
  429.5 11.2 %all-gather.2.cloned.1.call-done = bf16[2048,8192]{1,0:T(8,128)(2,1)} async-done(((bf16[256,8192]{1,0:T(8,128)(2,1)}), bf16[2048,8192]{1,0:T(8,128)(2,1)}) %all-gather.2.cloned.1.call-update) | async-done | bytes 33554448 | tf_op jit(solution)/shard_map/all_gather | solution.py:11
  440.7 44.7 %add_convert_fusion = bf16[8,256,1024]{2,1,0:T(8,128)(2,1)} fusion(bf16[8,256,1024]{2,1,0:T(8,128)(2,1)} %param.5, bf16[8,256,8192]{2,1,0:T(8,128)(2,1)} %bitcast.22, bf16[8192,1024,1]{1,0,2:T(8,128)(2,1)} %bitcast.18), kind=kOutput, calls=%fused_computation.1 | convolution fusion | flops 34366029824 | bytes 58720256 | tf_op jit(solution)/shard_map/dot_general | solution.py:10
Async XLA Ops:
  6.5 434.2 %all-gather.2.cloned.1.call-start = ((), (), s32[]{:S(2)}) async-start(), calls=%async_computation.2 | async-start | bytes 37748736 | tf_op jit(solution)/shard_map/all_gather | solution.py:11
Sparse Core Ops, SparseCore 0:
  108.5 332.2 all-gather.1
where the time goes:
time: 493 us; the launch traced here: 492 us
  blocking collectives  412 us (84%)
  matrix products  44.7 us (9%)
  between operations  13.4 us (3%)
  local copies, waits for them, and re-layouts  11.3 us (2%)
  waiting for transfers between devices  11.2 us (2%)
    all_to_all x1, blocking collectives, shards(): lax.all_to_all(out_weight, 'dp', split_axis=1, concat_axis=0, tiled=True)  312 us
    all_to_all x1, blocking collectives, shards(): lax.all_to_all(attn_out, 'mp', split_axis=0, concat_axis=1, tiled=True)  99.5 us
    dot_general x1, matrix products, shards(): jnp.dot(lax.all_gather(by_rows, 'dp', axis=0, tiled=True), columns, prefe...  44.7 us
    all_gather x1, waiting for transfers between devices, shards(): lax.all_gather(by_rows, 'dp', axis=0, tiled=True)  11.2 us
  transfers between devices with their start and end apart: 1, of which 1 were waited for; matrix products, arithmetic and copies ran while one was open for 2% of the time, Pallas kernels for 0%

commit v1 on v0

--- a/solution.py
+++ b/solution.py
@@ -5,7 +5,9 @@
 
 
 def shards(attn_out, out_weight, residual):
-    by_rows = lax.all_to_all(attn_out, "mp", split_axis=0, concat_axis=1, tiled=True)
+    cells = jnp.split(attn_out, lax.axis_size("mp"), axis=0)
+    received = lax.all_to_all(jnp.stack(cells), "mp", 0, 0)
+    by_rows = jnp.concatenate(received, axis=1)
     columns = lax.all_to_all(out_weight, "dp", split_axis=1, concat_axis=0, tiled=True)
     projected = jnp.dot(
         lax.all_gather(by_rows, "dp", axis=0, tiled=True),

time: 493 us -> 550 us (1.12)
  blocking collectives: 412 us -> 99.4 us
  waiting for transfers between devices: 11.2 us -> 319 us
  local copies, waits for them, and re-layouts: 11.3 us -> 64.5 us
  starting transfers between devices: 0.01 us -> 5.82 us
    all_to_all x2 -> x1, blocking collectives: 412 us -> 99.4 us  [shards(): received = lax.all_to_all(jnp.stack(cells), 'mp', 0, 0)]
    all_gather x1, waiting for transfers between devices: 11.2 us -> 319 us  [shards(): lax.all_gather(by_rows, 'dp', axis=0, tiled=True)]
    all_gather x0 -> x1, local copies, waits for them, and re-layouts: none -> 40.5 us  [shards(): lax.all_gather(by_rows, 'dp', axis=0, tiled=True)]
    all_to_all x0 -> x1, starting transfers between devices: none -> 5.81 us  [shards(): lax.all_to_all(out_weight, 'dp', split_axis=1, concat_axis=0, tiled=True)]
    unnamed x0 -> x4, local copies, waits for them, and re-layouts: none -> 5.57 us
    all_to_all x1, local copies, waits for them, and re-layouts: 9.01 us -> 14.5 us  [shards(): lax.all_to_all(out_weight, 'dp', split_axis=1, concat_axis=0, tiled=True)]
  transfers between devices with their start and end apart: 1 -> 2, of which waited for: 1 -> 1; matrix products, arithmetic and copies ran while one was open for 2% -> 10% of each run, Pallas kernels for 0% -> 0%
where the time goes in v1:
time: 550 us; the launch traced here: 548 us
  waiting for transfers between devices  319 us (58%)
  blocking collectives  99.4 us (18%)
  local copies, waits for them, and re-layouts  64.5 us (12%)
  matrix products  44.7 us (8%)
  between operations  13.4 us (2%)
  starting transfers between devices  5.82 us (1%)
    all_gather x1, waiting for transfers between devices, shards(): lax.all_gather(by_rows, 'dp', axis=0, tiled=True)  319 us
    all_to_all x1, blocking collectives, shards(): received = lax.all_to_all(jnp.stack(cells), 'mp', 0, 0)  99.4 us
    dot_general x1, matrix products, shards(): jnp.dot(lax.all_gather(by_rows, 'dp', axis=0, tiled=True), columns, prefe...  44.7 us
    all_gather x1, local copies, waits for them, and re-layouts, shards(): lax.all_gather(by_rows, 'dp', axis=0, tiled=True)  40.5 us
    all_to_all x1, local copies, waits for them, and re-layouts, shards(): lax.all_to_all(out_weight, 'dp', split_axis=1, concat_axis=0, tiled=True)  14.5 us
  transfers between devices with their start and end apart: 2, of which 1 were waited for; matrix products, arithmetic and copies ran while one was open for 10% of the time, Pallas kernels for 0%

profile of v1, /device:TPU:0, one launch (start us, length us, event | category | flops | bytes accessed | tf_op | source)
XLA Modules:
  0.0 548.2 jit_solution(10985900626313082089)
XLA Ops:
  6.5 0.0 all-gather.2.cloned.1.call-start
  6.5 3.9 fusion
  10.5 0.5 copy.11
  11.0 1.5 copy.13
  12.5 2.3 copy.12
  14.8 1.3 copy.14
  16.1 1.8 pad_maximum_fusion
  17.9 99.4 %all_to_all.24 = bf16[4,256,2048]{1,2,0:T(8,128)(2,1)} all-to-all(bf16[4,256,2048]{1,2,0:T(8,128)(2,1)S(1)} %pad_maximum_fusion), channel_id=1, replica_groups=mesh['dp'=8,'mp'=4] {'mp'}, dimensions={0} | all-to-all | bytes 8388608 | tf_op jit(solution)/shard_map/all_to_all | solution.py:9
  117.3 0.0 all-gather.2.cloned.1.call-update
  117.3 14.5 %copy.17 = bf16[128,8,8,1024]{3,2,0,1:T(8,128)(2,1)} copy(bf16[128,8,8,1024]{3,2,1,0:T(8,128)(2,1)} %bitcast.21) | data formatting | bytes 33554432 | tf_op jit(solution)/shard_map/all_to_all | solution.py:11
  131.8 5.8 %all-to-all-start.1 = ((bf16[1024,8,1024]{2,0,1:T(8,128)(2,1)}), bf16[1024,8,1024]{2,0,1:T(8,128)(2,1)}, u32[]{:S(2)}, u32[]{:S(2)}) async-start(bf16[1024,8,1024]{2,0,1:T(8,128)(2,1)} %bitcast.19), calls=%async_computation.1 | async-start | bytes 33554432 | tf_op jit(solution)/shard_map/all_to_all | solution.py:11
  137.6 318.6 %all-gather.2.cloned.1.call-done = bf16[2048,8192]{0,1:T(8,128)(2,1)} async-done(((bf16[256,8192]{0,1:T(8,128)(2,1)}), bf16[2048,8192]{0,1:T(8,128)(2,1)}) %all-gather.2.cloned.1.call-update) | async-done | bytes 33554448 | tf_op jit(solution)/shard_map/all_gather | solution.py:13
  456.2 40.5 %copy.9 = bf16[2048,8192]{1,0:T(8,128)(2,1)} copy(bf16[2048,8192]{0,1:T(8,128)(2,1)} %all-gather.2.cloned.1.call-done) | data formatting | bytes 67108864 | tf_op jit(solution)/shard_map/all_gather | solution.py:13
  496.7 0.0 all-to-all-done.1
  496.7 44.7 %add_convert_fusion = bf16[8,256,1024]{2,1,0:T(8,128)(2,1)} fusion(bf16[8,256,1024]{2,1,0:T(8,128)(2,1)} %param.5, bf16[8,256,8192]{2,1,0:T(8,128)(2,1)} %bitcast.20, bf16[8192,1024,1]{1,0,2:T(8,128)(2,1)} %bitcast.9), kind=kOutput, calls=%fused_computation.1 | convolution fusion | flops 34366029824 | bytes 58720256 | tf_op jit(solution)/shard_map/dot_general | solution.py:12
Async XLA Ops:
  6.5 449.7 %all-gather.2.cloned.1.call-start = ((), (), s32[]{:S(2)}) async-start(), calls=%async_computation.2 | async-start | bytes 37748736 | tf_op jit(solution)/shard_map/all_gather | solution.py:13
  131.8 364.9 %all-to-all-start.1 = ((bf16[1024,8,1024]{2,0,1:T(8,128)(2,1)}), bf16[1024,8,1024]{2,0,1:T(8,128)(2,1)}, u32[]{:S(2)}, u32[]{:S(2)}) async-start(bf16[1024,8,1024]{2,0,1:T(8,128)(2,1)} %bitcast.19), calls=%async_computation.1 | async-start | bytes 33554432 | tf_op jit(solution)/shard_map/all_to_all | solution.py:11
Sparse Core Ops, SparseCore 0:
  117.4 338.7 all-gather.1
